TPU v7x, 32 devices: a whole 2x2x4 slice. The times are simulated.
32 devices in a mesh: row: 8 (over y, x, core), col: 4 (over z).
Axes of the slice: x: 2, y: 2, z: 4, core: 2. Of those that a mesh axis runs over, the one named last changes fastest.
Arguments:
- tangents: float32 [192, 128, 6144], P('row', None, 'col'), may hold values from -6 to 6
- base_flow: float32 [192, 128, 192], P('row', None, 'col'), may hold values from -0.0625 to 0.0625
- mode_mask: int32 [192, 192], P('row', 'col'), may hold values 0 or 1
- decay_rates: float32 [128], replicated, may hold values from 1 to 100
- to_eigen: float32 [128, 128], replicated, may hold values from -0.5 to 0.5
- from_eigen: float32 [128, 128], replicated, may hold values from -0.5 to 0.5
Outputs:
- vectors: float32 [192, 128, 6144], P('row', None, 'col')
- growth: float32 [32], replicated
Inputs may be any that keep to these rules, and one draw needn't show every extreme that they name: `mode_mask`: 1 keeps a mode pair of the linearized product, 0 removes it.
All inputs are finite; a program needn't handle non-finite values. No bound on the sum of `mode_mask` on one device may be relied on, other than what follows from the above.
Results may differ from a plain program's by a relative error of at most 0.00005.
Values sent between devices are 32-bit elements; how exact they have to be, the bound alone decides.
A program may use at most 256 MiB of HBM per device.

v0:
```python
import math
import jax
import jax.numpy as jnp
from jax import lax
from jax.sharding import PartitionSpec as P

PRECISE = lax.Precision.HIGHEST
STEP_COEF = 10.0
VISCOSITY = 0.01
ALPHA_X = 0.5
BETA_Z = 1.0


def local_waves(points_count, first_index, length):
    indices = first_index + jnp.arange(length, dtype=jnp.int32)
    middle = points_count // 2
    return jnp.where(indices <= middle, indices, indices - middle).astype(jnp.float32)


def synthesis(points_count):
    points = jnp.arange(points_count, dtype=jnp.int32)[:, None]
    mode_index = jnp.arange(points_count, dtype=jnp.int32)[None, :]
    middle = points_count // 2
    wave_index = jnp.where(mode_index <= middle, mode_index, mode_index - middle)
    turn_count = (points * wave_index % points_count).astype(jnp.float32)
    angles = turn_count * (2.0 * math.pi / points_count)
    return jnp.where(mode_index <= middle, jnp.cos(angles), jnp.sin(angles))


def analysis(points_count):
    mode_index = jnp.arange(points_count, dtype=jnp.int32)
    middle = points_count // 2
    weights = jnp.where(
        (mode_index == 0) | (mode_index == middle),
        jnp.float32(1.0 / points_count),
        jnp.float32(2.0 / points_count),
    )
    return weights[:, None] * synthesis(points_count).T


def derivative_analysis(points_count, wave_scale):
    rows_index = jnp.arange(points_count, dtype=jnp.int32)[:, None]
    cols_index = jnp.arange(points_count, dtype=jnp.int32)[None, :]
    middle = points_count // 2
    rising = (cols_index == rows_index + middle) & (rows_index >= 1) & (rows_index < middle)
    falling = (rows_index == cols_index + middle) & (cols_index >= 1) & (cols_index < middle)
    rows_float = jnp.broadcast_to(rows_index.astype(jnp.float32), (points_count, points_count))
    cols_float = jnp.broadcast_to(cols_index.astype(jnp.float32), (points_count, points_count))
    derivative = jnp.where(rising, rows_float, jnp.float32(0.0)) - jnp.where(
        falling, cols_float, jnp.float32(0.0)
    )
    return -wave_scale * jnp.dot(derivative, analysis(points_count), precision=PRECISE)


def denominators(decay_rates, x_count, z_count, x_start, z_start, x_length, z_length):
    wave_x = ALPHA_X * local_waves(x_count, x_start, x_length)
    wave_z = BETA_Z * local_waves(z_count, z_start, z_length)
    return (
        STEP_COEF
        + VISCOSITY * (wave_x[:, None, None] ** 2 + wave_z[None, None, :] ** 2)
        + decay_rates[None, :, None]
    )


def body(tangents, base_flow, mode_mask, decay_rates, to_eigen, from_eigen):
    x_length, y_count, zv_length = tangents.shape
    z_length = base_flow.shape[2]
    vec_count = zv_length // z_length
    row_devices = lax.axis_size("row")
    col_devices = lax.axis_size("col")
    x_count = x_length * row_devices
    z_count = z_length * col_devices
    x_synthesis = synthesis(x_count)
    z_synthesis = synthesis(z_count)
    x_derivative = derivative_analysis(x_count, ALPHA_X)
    z_analysis = analysis(z_count)
    all_devices = row_devices * col_devices
    plane_count = y_count // all_devices
    stacked = tangents.reshape(x_length, y_count, 1, zv_length)
    speed_stack = base_flow.reshape(x_length, y_count, 1, z_length)
    planes, speed_field = (
        lax.all_to_all(stacked, ("row", "col"), split_axis=1, concat_axis=2, tiled=True),
        lax.all_to_all(speed_stack, ("row", "col"), split_axis=1, concat_axis=2, tiled=True),
    )
    x_table = x_synthesis.reshape(x_count, row_devices, x_length)
    z_table = z_synthesis.reshape(z_count, col_devices, z_length)
    planes = planes.reshape(x_length, plane_count, row_devices, col_devices, z_length, vec_count)
    physical = jnp.einsum("myrcnv,prm->ypcnv", planes, x_table, precision=PRECISE)
    physical = jnp.einsum("ypcnv,scn->ypsv", physical, z_table, precision=PRECISE)
    speed_field = speed_field.reshape(x_length, plane_count, row_devices, col_devices, z_length)
    speed_field = jnp.einsum("myrcn,prm->ypcn", speed_field, x_table, precision=PRECISE)
    speed_field = jnp.einsum("ypcn,scn->yps", speed_field, z_table, precision=PRECISE)
    product = physical * speed_field[:, :, :, None]
    returned = jnp.einsum("ypsv,ns->ypnv", product, z_analysis, precision=PRECISE)
    returned = jnp.einsum("ypnv,mp->ymnv", returned, x_derivative, precision=PRECISE)
    returned = returned.reshape(
        plane_count, row_devices, x_length, col_devices, z_length, vec_count
    )
    returned = jnp.transpose(returned, (2, 0, 1, 3, 4, 5)).reshape(
        x_length, plane_count, all_devices, zv_length
    )
    nonlinear = lax.all_to_all(returned, ("row", "col"), split_axis=2, concat_axis=1, tiled=True)
    nonlinear = nonlinear.reshape(x_length, y_count, zv_length)
    x_start = lax.axis_index("row") * x_length
    z_start = lax.axis_index("col") * z_length
    divisor = denominators(decay_rates, x_count, z_count, x_start, z_start, x_length, z_length)
    retained = mode_mask.astype(jnp.float32)[:, None, :, None]
    nonlinear = nonlinear.reshape(x_length, y_count, z_length, vec_count) * retained
    right_side = STEP_COEF * tangents.reshape(x_length, y_count, z_length, vec_count) + nonlinear
    eigen_part = jnp.einsum(
        "ji,mic->mjc", to_eigen, right_side.reshape(x_length, y_count, zv_length), precision=PRECISE
    )
    eigen_part = eigen_part.reshape(x_length, y_count, z_length, vec_count) / divisor[:, :, :, None]
    stepped = jnp.einsum(
        "yj,mjc->myc",
        from_eigen,
        eigen_part.reshape(x_length, y_count, zv_length),
        precision=PRECISE,
    )
    columns = stepped.reshape(x_length * y_count * z_length, vec_count)
    cell_count = x_count * y_count * z_count
    identity = jnp.eye(vec_count, dtype=jnp.float32)

    def refine(block):
        local_gram = jnp.einsum("cv,cu->vu", block, block, precision=PRECISE)
        gram_matrix = lax.psum(local_gram, ("row", "col")) / cell_count
        lower_factor = jnp.linalg.cholesky(gram_matrix)
        inverse = jax.scipy.linalg.solve_triangular(lower_factor, identity, lower=True)
        refined = jnp.einsum("cv,uv->cu", block, inverse, precision=PRECISE)
        return (refined, jnp.log(jnp.diagonal(lower_factor)))

    first_pass, first_growth = refine(columns)
    orthonormal, second_growth = refine(first_pass)
    growth = first_growth + second_growth
    return (orthonormal.reshape(x_length, y_count, zv_length), growth)


def solution(mesh):
    placed = (P("row", None, "col"), P("row", None, "col"), P("row", "col"), P(), P(), P())
    return jax.shard_map(
        body, mesh=mesh, in_specs=placed, out_specs=(P("row", None, "col"), P()), check_vma=False
    )
```

profile of v0, /device:TPU:0, one launch (start us, length us, event | category | flops | bytes accessed | tf_op | source)
XLA Modules:
  0.0 2041.6 jit_solution(13407496623339631732)
XLA Ops:
  0.6 0.0 copy-start
  0.6 1.6 copy.62
  2.3 0.1 bitcast_bitcast_fusion
  2.4 2.4 reshape.235
  4.8 7.3 all-to-all-start.1
  12.1 19.6 copy.107
  31.7 0.0 all-to-all-done.1
  31.7 6.1 all-to-all-start
  38.0 1.3 fusion.19
  39.3 0.9 fusion.148
  40.2 0.5 broadcast.375
  40.7 2.0 reduce.4
  42.7 0.7 reshape.236
  43.4 3.4 fusion.16
  46.8 1.7 convolution_bitcast_fusion.1
  48.5 394.0 %all-to-all-done = f32[24,128,1,1536]{3,0,2,1:T(8,128)} async-done(((f32[24,128,1,1536]{3,0,2,1:T(8,128)}), f32[24,128,1,1536]{3,0,2,1:T(8,128)}, u32[]{:S(2)}, u32[]{:S(2)}) %all-to-all-start) | async-done | bytes 18874400 | tf_op jit(solution)/shard_map/all_to_all | solution.py:82
  442.5 19.6 copy.106
  462.2 44.8 %reshape.204 = f32[24,4,8,4,48,32]{5,4,3,2,1,0:T(8,128)} reshape(f32[24,4,32,1,1536]{4,2,1,0,3:T(8,128)} %bitcast.144) | data formatting | bytes 37748736 | tf_op jit(solution)/shard_map/reshape | solution.py:87
  507.0 67.4 %copy.60 = f32[24,4,8,4,48,32]{4,0,2,5,3,1:T(8,128)} copy(f32[24,4,8,4,48,32]{5,4,3,2,1,0:T(8,128)} %reshape.204) | data formatting | bytes 37748736 | tf_op jit(solution)/shard_map/reshape | solution.py:87
  574.4 86.3 %fusion.28 = f32[192,4,4,48,32,1]{0,3,5,4,2,1:T(8,128)} fusion(f32[24,4,8,4,48,32]{4,0,2,5,3,1:T(8,128)} %copy.60, f32[192,8,24,1,1,1]{0,2,1,5,4,3:T(8,128)S(1)} %fusion.148), kind=kOutput, calls=%fused_computation.36 | convolution fusion | flops 10871635968 | bytes 37896192 | tf_op jit(solution)/shard_map/myrcnv,prm->ypcnv/dot_general | solution.py:88
  660.7 31.7 %fusion.1 = f32[192,4,192,32,1]{2,0,3,4,1:T(8,128)} fusion(f32[192,4,4,48,32,1]{0,3,5,4,2,1:T(8,128)} %fusion.28, s32[4,48]{1,0:T(4,128)S(1)} %add_select_fusion.4, pred[4,48]{1,0:T(4,128)(4,1)S(1)} %fusion.103), kind=kOutput, calls=%fused_computation.4 | convolution fusion | flops 10872004608 | bytes 37749696 | tf_op jit(solution)/shard_map/ypcnv,scn->ypsv/dot_general | solution.py:89
  692.4 30.9 %fusion = f32[192,4,192,32]{2,0,3,1:T(8,128)} fusion(f32[192,4,192,32,1]{2,0,3,4,1:T(8,128)} %fusion.1, f32[4,192,192]{1,2,0:T(8,128)S(1)} %convolution_bitcast_fusion.1, s32[192]{0:T(256)S(1)} %get-tuple-element.8, f32[192]{0:T(256)S(1)} %or_select_fusion, pred[192]{0:T(512)(128)(4,1)S(1)} %get-tuple-element.10), kind=kOutput, calls=%fused_computation.3 | convolution fusion | flops 10876760064 | bytes 38340288 | tf_op jit(solution)/shard_map/ypsv,ns->ypnv/dot_general | solution.py:94
  723.3 28.1 %fusion.9 = f32[4,192,192,32]{2,1,3,0:T(8,128)} fusion(f32[192,192,1,1]{1,0,3,2:T(8,128)S(1)} %fusion.19, f32[192,4,192,32]{2,0,3,1:T(8,128)} %fusion), kind=kOutput, calls=%fused_computation.16 | convolution fusion | flops 10871635968 | bytes 37896192 | tf_op jit(solution)/shard_map/ypnv,mp->ymnv/dot_general | solution.py:95
  751.4 44.9 %reshape.207 = f32[4,8,24,4,48,32]{4,3,2,1,5,0:T(4,128)} reshape(f32[4,192,192,32]{2,1,3,0:T(8,128)} %fusion.9) | data formatting | bytes 37748736 | tf_op jit(solution)/shard_map/reshape | solution.py:96
  796.3 71.3 %copy.68 = f32[4,8,24,4,48,32]{5,4,3,1,0,2:T(8,128)} copy(f32[4,8,24,4,48,32]{4,3,2,1,5,0:T(4,128)} %reshape.207) | data formatting | bytes 37748736 | tf_op jit(solution)/shard_map/reshape | solution.py:96
  867.7 53.6 %reshape.208 = f32[24,4,32,1536]{3,2,1,0:T(8,128)} reshape(f32[24,4,8,4,48,32]{5,4,3,2,1,0:T(8,128)} %bitcast.33) | data formatting | bytes 37748736 | tf_op jit(solution)/shard_map/reshape | solution.py:99
  921.3 23.2 %copy.69 = f32[24,4,32,1536]{3,1,0,2:T(4,128)} copy(f32[24,4,32,1536]{3,2,1,0:T(8,128)} %reshape.208) | data formatting | bytes 37748736 | tf_op jit(solution)/shard_map/reshape | solution.py:99
  944.5 17.9 all-to-all-start.2
  962.4 0.0 copy-done.4
  962.5 0.2 mul.165
  962.7 0.3 mul.166
  962.9 0.5 or_bitcast_fusion
  963.5 0.1 multiply_add_fusion
  963.5 0.2 broadcast_add_fusion
  963.8 403.4 %all-to-all-done.2 = f32[24,4,32,1536]{3,1,0,2:T(4,128)} async-done(((f32[24,4,32,1536]{3,1,0,2:T(4,128)}), f32[24,4,32,1536]{3,1,0,2:T(4,128)}, u32[]{:S(2)}, u32[]{:S(2)}) %all-to-all-start.2) | async-done | bytes 18874400 | tf_op jit(solution)/shard_map/all_to_all | solution.py:102
  1367.1 12.1 copy.70
  1379.2 20.4 %fusion.5 = f32[24,128,1536]{2,0,1:T(8,128)} fusion(f32[24,4,32,1536]{3,0,1,2:T(8,128)S(1)} %copy.70, f32[24,128,1536]{2,1,0:T(8,128)} %param.9, f32[24,1536]{1,0:T(8,128)S(1)} %mul.166), kind=kLoop, calls=%fused_computation.9 | loop fusion | flops 14155776 | bytes 56770560 | tf_op jit(solution)/shard_map/add | solution.py:109
  1399.7 38.5 %bitcast_divide_fusion = f32[24,128,1536]{1,2,0:T(8,128)S(1)} fusion(f32[24,128,48]{1,2,0:T(8,128)S(1)} %broadcast_add_fusion, f32[24,128,1536]{2,0,1:T(8,128)} %fusion.5, f32[128,128]{1,0:T(8,128)S(1)} %copy-done), kind=kOutput, calls=%fused_computation.10 | convolution fusion | flops 7252475904 | bytes 38404096 | tf_op jit(solution)/shard_map/ji,mic->mjc/dot_general | solution.py:110
  1438.2 0.0 copy-done.3
  1438.2 17.9 convolution_bitcast_fusion
  1456.1 18.7 copy.72
  1474.8 44.8 %reshape.209 = f32[147456,32]{1,0:T(8,128)} reshape(f32[24,128,1536]{2,1,0:T(8,128)} %copy.72) | data formatting | bytes 37748736 | tf_op jit(solution)/shard_map/reshape | solution.py:120
  1519.6 129.6 %fusion.129 = f32[32,32]{0,1:T(8,128)S(1)} fusion(f32[147456,32]{1,0:T(8,128)} %reshape.209), kind=kOutput, calls=%fused_computation.172 | convolution fusion | flops 1811939328 | bytes 18878464 | tf_op jit(solution)/shard_map/cv,cu->vu/dot_general | solution.py:125
  1649.2 53.2 %psum.14 = f32[32,32]{0,1:T(8,128)S(1)} all-reduce(f32[32,32]{0,1:T(8,128)S(1)} %fusion.129), channel_id=1, replica_groups=mesh['row'=8,'col'=4] {'row','col'}, use_global_device_ids=true, to_apply=%region_0.1 | all-reduce | flops 1024 | bytes 8192 | tf_op jit(solution)/shard_map/psum | solution.py:126
  1702.4 0.1 copy.74
  1702.5 2.9 cholesky.44
  1705.5 0.6 compare_reduce_fusion.1
  1706.1 0.7 select_bitcast_fusion.1
  1706.8 2.4 custom-call.10
  1709.2 0.2 fusion.95
  1709.4 85.6 %fusion.130 = f32[147456,32]{0,1:T(8,128)} fusion(f32[147456,32]{1,0:T(8,128)} %reshape.209, f32[32,32]{1,0:T(8,128)S(1)} %fusion.95), kind=kOutput, calls=%fused_computation.173 | convolution fusion | flops 1811939328 | bytes 37752832 | tf_op jit(solution)/shard_map/cv,uv->cu/dot_general | solution.py:129
  1795.0 19.3 fusion.131
  1814.4 39.5 %psum.15 = f32[32,32]{0,1:T(8,128)S(1)} all-reduce(f32[32,32]{0,1:T(8,128)S(1)} %fusion.131), channel_id=1, replica_groups=mesh['row'=8,'col'=4] {'row','col'}, use_global_device_ids=true, to_apply=%region_3.6 | all-reduce | flops 1024 | bytes 8192 | tf_op jit(solution)/shard_map/psum | solution.py:126
  1853.9 0.1 copy.76
  1854.0 2.9 cholesky.55
  1856.9 0.6 compare_reduce_fusion
  1857.6 0.7 select_bitcast_fusion
  1858.2 0.7 gather_fusion.1
  1859.0 0.7 gather_fusion
  1859.7 2.4 custom-call.11
  1862.1 0.2 fusion.93
  1862.3 124.7 %fusion.132 = f32[147456,32]{1,0:T(8,128)} fusion(f32[147456,32]{0,1:T(8,128)} %fusion.130, f32[32,32]{1,0:T(8,128)S(1)} %fusion.93), kind=kOutput, calls=%fused_computation.175 | convolution fusion | flops 1811939328 | bytes 37752832 | tf_op jit(solution)/shard_map/cv,uv->cu/dot_general | solution.py:129
  1987.1 53.6 %reshape.210 = f32[24,128,1536]{2,1,0:T(8,128)} reshape(f32[147456,32]{1,0:T(8,128)} %fusion.132) | data formatting | bytes 37748736 | tf_op jit(solution)/shard_map/reshape | solution.py:135
  2040.7 0.5 log_add_fusion
  (27 shorter events, 0.2 us)
Async XLA Ops:
  0.6 1399.0 %copy-start = (f32[128,128]{1,0:T(8,128)S(1)}, f32[128,128]{1,0:T(8,128)}, u32[]{:S(2)}) copy-start(f32[128,128]{1,0:T(8,128)} %param.13) | copy-start | bytes 196612
  4.8 27.0 %all-to-all-start.1 = ((f32[32,1,4608]{2,1,0:T(1,128)}), f32[32,1,4608]{2,1,0:T(1,128)S(1)}, u32[]{:S(2)}, u32[]{:S(2)}) async-start(f32[32,1,4608]{2,1,0:T(1,128)} %reshape.235), calls=%async_computation.1 | async-start | bytes 1179648 | tf_op jit(solution)/shard_map/all_to_all | solution.py:83
  31.7 410.8 %all-to-all-start = ((f32[24,128,1,1536]{3,0,2,1:T(8,128)}), f32[24,128,1,1536]{3,0,2,1:T(8,128)}, u32[]{:S(2)}, u32[]{:S(2)}) async-start(f32[24,128,1,1536]{3,0,2,1:T(8,128)} %bitcast.143), calls=%async_computation | async-start | bytes 37748736 | tf_op jit(solution)/shard_map/all_to_all | solution.py:82
  944.5 17.9 copy-start.4
  944.5 19.0 copy-start.5
  944.5 422.6 %all-to-all-start.2 = ((f32[24,4,32,1536]{3,1,0,2:T(4,128)}), f32[24,4,32,1536]{3,1,0,2:T(4,128)}, u32[]{:S(2)}, u32[]{:S(2)}) async-start(f32[24,4,32,1536]{3,1,0,2:T(4,128)} %copy.69), calls=%async_computation.2 | async-start | bytes 37748736 | tf_op jit(solution)/shard_map/all_to_all | solution.py:102
  1399.7 38.5 %copy-start.3 = (f32[128,128]{1,0:T(8,128)S(1)}, f32[128,128]{1,0:T(8,128)}, u32[]{:S(2)}) copy-start(f32[128,128]{1,0:T(8,128)} %param.14) | copy-start | bytes 196612
  1795.0 63.2 %copy-start.2 = (s32[32]{0:T(128)S(1)}, s32[32]{0:T(128)}, u32[]{:S(2)}) copy-start(s32[32]{0:T(128)} %or_bitcast_fusion) | copy-start | bytes 388
  1987.1 54.1 %copy-start.1 = (f32[128,128]{1,0:T(8,128)S(1)}, f32[128,128]{1,0:T(8,128)}, u32[]{:S(2)}) copy-start(f32[128,128]{1,0:T(8,128)} %param.13) | copy-start | bytes 196612
where the time goes:
time: 2060 us; the launch traced here: 2040 us
  waiting for transfers between devices  797 us (39%)
  matrix products  600 us (29%)
  local copies, waits for them, and re-layouts  481 us (23%)
  blocking collectives  92.7 us (4%)
  other arithmetic  38.1 us (2%)
  starting transfers between devices  31.4 us (2%)
    all_to_all x1, waiting for transfers between devices, body(): lax.all_to_all(returned, ('row', 'col'), split_axis=2, concat_axis=1, til...  403 us
    all_to_all x1, waiting for transfers between devices, body(): lax.all_to_all(stacked, ('row', 'col'), split_axis=1, concat_axis=2, tile...  394 us
    dot_general x2, matrix products, refine(): refined = jnp.einsum('cv,uv->cu', block, inverse, precision=PRECISE)  210 us
    dot_general x2, matrix products, refine(): local_gram = jnp.einsum('cv,cu->vu', block, block, precision=PRECISE)  149 us
    reshape x2, local copies, waits for them, and re-layouts, body(): returned.reshape(plane_count, row_devices, x_length, col_devices, z_lengt...  116 us
    reshape x2, local copies, waits for them, and re-layouts, body(): planes.reshape(x_length, plane_count, row_devices, col_devices, z_length,...  112 us
    psum x2, blocking collectives, refine(): gram_matrix = lax.psum(local_gram, ('row', 'col')) / cell_count  92.7 us
    dot_general x1, matrix products, body(): jnp.einsum('myrcnv,prm->ypcnv', planes, x_table, precision=PRECISE)  86.3 us
  transfers between devices with their start and end apart: 3, of which 2 were waited for; matrix products, arithmetic and copies ran while one was open for 2% of the time, Pallas kernels for 0%

commit v1 on v0

--- a/solution.py
+++ b/solution.py
@@ -1,3 +1,4 @@
+import functools
 import math
 import jax
 import jax.numpy as jnp
@@ -9,6 +10,19 @@
 VISCOSITY = 0.01
 ALPHA_X = 0.5
 BETA_Z = 1.0
+
+
+def _supply_ratios(target, which_dim, along_dim):
+    local_now = lax.all_to_all(
+        jnp.stack(jnp.split(target, lax.axis_size(("row", "col")), axis=which_dim)),
+        ("row", "col"),
+        0,
+        0,
+    )
+    return jnp.concatenate(local_now, axis=along_dim)
+
+
+clusters_register = functools.partial(_supply_ratios, which_dim=2, along_dim=1)
 
 
 def local_waves(points_count, first_index, length):
@@ -99,7 +113,7 @@
     returned = jnp.transpose(returned, (2, 0, 1, 3, 4, 5)).reshape(
         x_length, plane_count, all_devices, zv_length
     )
-    nonlinear = lax.all_to_all(returned, ("row", "col"), split_axis=2, concat_axis=1, tiled=True)
+    nonlinear = clusters_register(returned)
     nonlinear = nonlinear.reshape(x_length, y_count, zv_length)
     x_start = lax.axis_index("row") * x_length
     z_start = lax.axis_index("col") * z_length

time: 2060 us -> 2160 us (1.049)
  local copies, waits for them, and re-layouts: 481 us -> 578 us
    unnamed x17 -> x48, local copies, waits for them, and re-layouts: 24.4 us -> 140 us
    reshape x2 -> x1, local copies, waits for them, and re-layouts: 76.8 us -> 53.8 us  [body(): jnp.transpose(returned, (2, 0, 1, 3, 4, 5))]
  transfers between devices with their start and end apart: 3 -> 3, of which waited for: 2 -> 2; matrix products, arithmetic and copies ran while one was open for 2% -> 1% of each run, Pallas kernels for 0% -> 0%
where the time goes in v1:
time: 2160 us; the launch traced here: 2150 us
  waiting for transfers between devices  797 us (37%)
  matrix products  611 us (28%)
  local copies, waits for them, and re-layouts  578 us (27%)
  blocking collectives  92.7 us (4%)
  other arithmetic  38.1 us (2%)
  starting transfers between devices  31.1 us (1%)
    all_to_all x1, waiting for transfers between devices, _supply_ratios(): lax.all_to_all(jnp.stack(jnp.split(target, lax.axis_size(('row', 'col')),...  403 us
    all_to_all x1, waiting for transfers between devices, body(): lax.all_to_all(stacked, ('row', 'col'), split_axis=1, concat_axis=2, tile...  394 us
    dot_general x2, matrix products, refine(): refined = jnp.einsum('cv,uv->cu', block, inverse, precision=PRECISE)  210 us
    dot_general x2, matrix products, refine(): local_gram = jnp.einsum('cv,cu->vu', block, block, precision=PRECISE)  149 us
    unnamed x48, local copies, waits for them, and re-layouts  140 us
    reshape x2, local copies, waits for them, and re-layouts, body(): returned.reshape(plane_count, row_devices, x_length, col_devices, z_lengt...  116 us
    reshape x2, local copies, waits for them, and re-layouts, body(): planes.reshape(x_length, plane_count, row_devices, col_devices, z_length,...  112 us
    dot_general x1, matrix products, body(): jnp.einsum('myrcnv,prm->ypcnv', planes, x_table, precision=PRECISE)  97.4 us
  transfers between devices with their start and end apart: 3, of which 2 were waited for; matrix products, arithmetic and copies ran while one was open for 1% of the time, Pallas kernels for 0%

profile of v1, /device:TPU:0, one launch (start us, length us, event | category | flops | bytes accessed | tf_op | source)
XLA Modules:
  0.0 2149.0 jit_solution(6921346409612188401)
XLA Ops:
  4.8 7.3 all-to-all-start.1
  12.1 19.6 copy.137
  31.7 6.2 all-to-all-start
  43.5 3.4 fusion.16
  48.6 394.0 %all-to-all-done = f32[24,128,1,1536]{3,0,2,1:T(8,128)} async-done(((f32[24,128,1,1536]{3,0,2,1:T(8,128)}), f32[24,128,1,1536]{3,0,2,1:T(8,128)}, u32[]{:S(2)}, u32[]{:S(2)}) %all-to-all-start) | async-done | bytes 18874400 | tf_op jit(solution)/shard_map/all_to_all | solution.py:96
  442.6 19.6 copy.136
  462.2 44.8 %reshape.206 = f32[24,4,8,4,48,32]{5,4,3,2,1,0:T(8,128)} reshape(f32[24,4,32,1,1536]{4,2,1,0,3:T(8,128)} %bitcast.269) | data formatting | bytes 37748736 | tf_op jit(solution)/shard_map/reshape | solution.py:101
  507.1 67.4 %copy.91 = f32[24,4,8,4,48,32]{4,0,2,5,3,1:T(8,128)} copy(f32[24,4,8,4,48,32]{5,4,3,2,1,0:T(8,128)} %reshape.206) | data formatting | bytes 37748736 | tf_op jit(solution)/shard_map/reshape | solution.py:101
  574.5 97.4 %fusion.60 = f32[192,4,4,48,32,1]{0,3,5,4,2,1:T(8,128)} fusion(f32[24,4,8,4,48,32]{4,0,2,5,3,1:T(8,128)} %copy.91, f32[192,8,24,1,1,1]{0,2,1,5,4,3:T(8,128)S(1)} %fusion.180), kind=kOutput, calls=%fused_computation.100 | convolution fusion | flops 10871635968 | bytes 37896192 | tf_op jit(solution)/shard_map/myrcnv,prm->ypcnv/dot_general | solution.py:102
  671.9 31.7 %fusion.1 = f32[192,4,192,32,1]{2,0,3,4,1:T(8,128)} fusion(f32[192,4,4,48,32,1]{0,3,5,4,2,1:T(8,128)} %fusion.60, s32[4,48]{1,0:T(4,128)S(1)} %add_select_fusion.4, pred[4,48]{1,0:T(4,128)(4,1)S(1)} %fusion.135), kind=kOutput, calls=%fused_computation.4 | convolution fusion | flops 10872004608 | bytes 37749696 | tf_op jit(solution)/shard_map/ypcnv,scn->ypsv/dot_general | solution.py:103
  703.6 30.9 %fusion = f32[192,4,192,32]{2,0,3,1:T(8,128)} fusion(f32[192,4,192,32,1]{2,0,3,4,1:T(8,128)} %fusion.1, f32[4,192,192]{1,2,0:T(8,128)S(1)} %convolution_bitcast_fusion.1, s32[192]{0:T(256)S(1)} %get-tuple-element.8, f32[192]{0:T(256)S(1)} %or_select_fusion, pred[192]{0:T(512)(128)(4,1)S(1)} %get-tuple-element.10), kind=kOutput, calls=%fused_computation.3 | convolution fusion | flops 10876760064 | bytes 38340288 | tf_op jit(solution)/shard_map/ypsv,ns->ypnv/dot_general | solution.py:108
  734.5 28.1 %fusion.9 = f32[4,192,192,32]{2,1,3,0:T(8,128)} fusion(f32[192,192,1,1]{1,0,3,2:T(8,128)S(1)} %fusion.19, f32[192,4,192,32]{2,0,3,1:T(8,128)} %fusion), kind=kOutput, calls=%fused_computation.16 | convolution fusion | flops 10871635968 | bytes 37896192 | tf_op jit(solution)/shard_map/ypnv,mp->ymnv/dot_general | solution.py:109
  762.5 44.9 %reshape.209 = f32[4,8,24,4,48,32]{4,3,2,1,5,0:T(4,128)} reshape(f32[4,192,192,32]{2,1,3,0:T(8,128)} %fusion.9) | data formatting | bytes 37748736 | tf_op jit(solution)/shard_map/reshape | solution.py:110
  807.5 71.3 %copy.99 = f32[4,8,24,4,48,32]{5,4,3,1,0,2:T(8,128)} copy(f32[4,8,24,4,48,32]{4,3,2,1,5,0:T(4,128)} %reshape.209) | data formatting | bytes 37748736 | tf_op jit(solution)/shard_map/reshape | solution.py:110
  878.8 53.8 %reshape.210 = f32[24,4,32,1536]{3,2,1,0:T(8,128)} reshape(f32[24,4,8,4,48,32]{5,4,3,2,1,0:T(8,128)} %bitcast.33) | data formatting | bytes 37748736 | tf_op jit(solution)/shard_map/reshape | solution.py:113
  932.6 3.5 fusion.51
  936.1 3.8 fusion.50
  939.9 3.8 fusion.49
  943.6 3.7 fusion.48
  947.4 3.7 fusion.47
  951.1 3.7 fusion.46
  954.9 3.7 fusion.45
  958.6 3.8 fusion.44
  962.4 3.5 fusion.43
  965.9 3.7 fusion.42
  969.6 3.8 fusion.41
  973.4 3.8 fusion.40
  977.2 3.8 fusion.39
  981.0 3.7 fusion.38
  984.7 3.8 fusion.37
  988.5 3.8 fusion.36
  992.2 3.5 fusion.35
  995.7 3.8 fusion.34
  999.5 3.8 fusion.33
  1003.3 3.8 fusion.32
  1007.0 4.2 fusion.31
  1011.3 3.8 fusion.30
  1015.0 3.7 fusion.29
  1018.8 3.7 fusion.28
  1022.5 3.5 fusion.27
  1026.0 3.8 fusion.26
  1029.8 3.8 fusion.25
  1033.5 3.8 fusion.24
  1037.3 3.7 fusion.23
  1041.0 3.8 fusion.22
  1044.8 3.7 fusion.21
  1048.5 3.8 fusion.20
  1052.3 17.5 all-to-all-start.2
  1071.2 403.4 %all-to-all-done.2 = f32[32,24,4,1,1536]{4,3,2,1,0:T(1,128)} async-done(((f32[32,24,4,1,1536]{4,3,2,1,0:T(1,128)}), f32[32,24,4,1,1536]{4,3,2,1,0:T(1,128)}, u32[]{:S(2)}, u32[]{:S(2)}) %all-to-all-start.2) | async-done | bytes 18874400 | tf_op jit(solution)/shard_map/all_to_all | solution.py:16
  1474.5 12.1 copy.100
  1486.7 20.4 fusion.5
  1507.1 38.5 %bitcast_divide_fusion = f32[24,128,1536]{1,2,0:T(8,128)S(1)} fusion(f32[24,128,48]{1,2,0:T(8,128)S(1)} %broadcast_add_fusion, f32[24,128,1536]{2,0,1:T(8,128)} %fusion.5, f32[128,128]{1,0:T(8,128)S(1)} %copy-done), kind=kOutput, calls=%fused_computation.8 | convolution fusion | flops 7252475904 | bytes 38404096 | tf_op jit(solution)/shard_map/ji,mic->mjc/dot_general | solution.py:124
  1545.6 17.9 convolution_bitcast_fusion
  1563.5 18.7 copy.102
  1582.2 44.8 %reshape.212 = f32[147456,32]{1,0:T(8,128)} reshape(f32[24,128,1536]{2,1,0:T(8,128)} %copy.102) | data formatting | bytes 37748736 | tf_op jit(solution)/shard_map/reshape | solution.py:134
  1627.0 129.6 %fusion.161 = f32[32,32]{0,1:T(8,128)S(1)} fusion(f32[147456,32]{1,0:T(8,128)} %reshape.212), kind=kOutput, calls=%fused_computation.236 | convolution fusion | flops 1811939328 | bytes 18878464 | tf_op jit(solution)/shard_map/cv,cu->vu/dot_general | solution.py:139
  1756.7 53.2 %psum.14 = f32[32,32]{0,1:T(8,128)S(1)} all-reduce(f32[32,32]{0,1:T(8,128)S(1)} %fusion.161), channel_id=1, replica_groups=mesh['row'=8,'col'=4] {'row','col'}, use_global_device_ids=true, to_apply=%region_0.1 | all-reduce | flops 1024 | bytes 8192 | tf_op jit(solution)/shard_map/psum | solution.py:140
  1810.0 2.9 cholesky.44
  1816.9 85.6 %fusion.162 = f32[147456,32]{0,1:T(8,128)} fusion(f32[147456,32]{1,0:T(8,128)} %reshape.212, f32[32,32]{1,0:T(8,128)S(1)} %fusion.127), kind=kOutput, calls=%fused_computation.237 | convolution fusion | flops 1811939328 | bytes 37752832 | tf_op jit(solution)/shard_map/cv,uv->cu/dot_general | solution.py:143
  1902.5 19.3 fusion.163
  1921.8 39.5 %psum.15 = f32[32,32]{0,1:T(8,128)S(1)} all-reduce(f32[32,32]{0,1:T(8,128)S(1)} %fusion.163), channel_id=1, replica_groups=mesh['row'=8,'col'=4] {'row','col'}, use_global_device_ids=true, to_apply=%region_3.6 | all-reduce | flops 1024 | bytes 8192 | tf_op jit(solution)/shard_map/psum | solution.py:140
  1961.4 2.9 cholesky.55
  1969.8 124.7 %fusion.164 = f32[147456,32]{1,0:T(8,128)} fusion(f32[147456,32]{0,1:T(8,128)} %fusion.162, f32[32,32]{1,0:T(8,128)S(1)} %fusion.125), kind=kOutput, calls=%fused_computation.239 | convolution fusion | flops 1811939328 | bytes 37752832 | tf_op jit(solution)/shard_map/cv,uv->cu/dot_general | solution.py:143
  2094.5 53.6 %reshape.213 = f32[24,128,1536]{2,1,0:T(8,128)} reshape(f32[147456,32]{1,0:T(8,128)} %fusion.164) | data formatting | bytes 37748736 | tf_op jit(solution)/shard_map/reshape | solution.py:149
  (58 shorter events, 22.7 us)
Async XLA Ops:
  0.6 1506.5 %copy-start = (f32[128,128]{1,0:T(8,128)S(1)}, f32[128,128]{1,0:T(8,128)}, u32[]{:S(2)}) copy-start(f32[128,128]{1,0:T(8,128)} %param.13) | copy-start | bytes 196612
  4.8 27.0 %all-to-all-start.1 = ((f32[32,1,4608]{2,1,0:T(1,128)}), f32[32,1,4608]{2,1,0:T(1,128)S(1)}, u32[]{:S(2)}, u32[]{:S(2)}) async-start(f32[32,1,4608]{2,1,0:T(1,128)} %reshape.238), calls=%async_computation.1 | async-start | bytes 1179648 | tf_op jit(solution)/shard_map/all_to_all | solution.py:97
  31.7 410.9 %all-to-all-start = ((f32[24,128,1,1536]{3,0,2,1:T(8,128)}), f32[24,128,1,1536]{3,0,2,1:T(8,128)}, u32[]{:S(2)}, u32[]{:S(2)}) async-start(f32[24,128,1,1536]{3,0,2,1:T(8,128)} %bitcast.268), calls=%async_computation | async-start | bytes 37748736 | tf_op jit(solution)/shard_map/all_to_all | solution.py:96
  1052.3 17.5 copy-start.4
  1052.3 18.6 copy-start.5
  1052.3 422.2 %all-to-all-start.2 = ((f32[32,24,4,1,1536]{4,3,2,1,0:T(1,128)}), f32[32,24,4,1,1536]{4,3,2,1,0:T(1,128)}, u32[]{:S(2)}, u32[]{:S(2)}) async-start(f32[32,24,4,1,1536]{4,3,2,1,0:T(1,128)} %fusion.20), calls=%async_computation.2 | async-start | bytes 37748736 | tf_op jit(solution)/shard_map/all_to_all | solution.py:16
  1507.1 38.5 %copy-start.3 = (f32[128,128]{1,0:T(8,128)S(1)}, f32[128,128]{1,0:T(8,128)}, u32[]{:S(2)}) copy-start(f32[128,128]{1,0:T(8,128)} %param.14) | copy-start | bytes 196612
  1902.5 63.2 %copy-start.2 = (s32[32]{0:T(128)S(1)}, s32[32]{0:T(128)}, u32[]{:S(2)}) copy-start(s32[32]{0:T(128)} %or_bitcast_fusion) | copy-start | bytes 388
  2094.5 54.1 %copy-start.1 = (f32[128,128]{1,0:T(8,128)S(1)}, f32[128,128]{1,0:T(8,128)}, u32[]{:S(2)}) copy-start(f32[128,128]{1,0:T(8,128)} %param.13) | copy-start | bytes 196612
